TPU v7x, 32 devices: a whole 2x2x4 slice. The times are simulated.
32 devices in a mesh: pipe: 4 (over x, core), mp: 8 (over z, y).
Axes of the slice: x: 2, y: 2, z: 4, core: 2. Of those that a mesh axis runs over, the one named last changes fastest.
Arguments:
- hidden_in: bfloat16 [32, 8192], P(None, 'mp'), may hold values from -24000 to 24000
- lengths: int32 [32], replicated, may hold values from 1 to 256
- assign: int32 [32], replicated, may hold values from 0 to 31, each once
- token_ids: int32 [32], replicated, may hold values from 0 to 12287
- attn_gain: bfloat16 [4, 8192], P('pipe', 'mp'), may hold values from 0.099609375 to 1.8984375
- qkv_weight: bfloat16 [4, 8192, 5120], P('pipe', 'mp'), may hold values from -0.0625 to 0.0625
- qkv_bias: bfloat16 [4, 5120], P('pipe'), may hold values from -3 to 3
- out_weight: bfloat16 [4, 4096, 8192], P('pipe', None, 'mp'), may hold values from -0.375 to 0.375
- kv_cache: bfloat16 [4, 32, 2, 4, 256, 128], P('pipe', 'mp'), may hold values from -120 to 120
- final_gain: bfloat16 [8192], P('mp'), may hold values from 0.099609375 to 1.8984375
- head_weight: bfloat16 [8192, 12288], P(None, ('pipe', 'mp')), may hold values from -0.9923308 to 0.9923308
Outputs:
- logprobs: float32 [32, 12288], P(None, ('pipe', 'mp'))
- chosen: float32 [32], replicated
Inputs may be any that keep to these rules, and one draw needn't show every extreme that they name: `assign`: a permutation of the 32 requests.
All inputs are finite; a program needn't handle non-finite values.
Results may differ from a plain program's by a relative error of at most 0.0017.
Values may be sent and summed in bfloat16 or wider, within the bound.
A program may use at most 64 MiB of HBM per device.

v0:
```python
import jax
import jax.numpy as jnp
from jax import lax
from jax.sharding import PartitionSpec as P

D = 8192
HEADS = 32
KV_HEADS = 4
HEAD_DIM = 128
MICRO = 4
MB_ROWS = 8


EPS = 1e-06
THETA = 1000000.0


def from_behind(block, axis, distance):
    devices = range(lax.axis_size(axis))
    route = [(i - distance, i) for i in devices if i - distance in devices]
    return lax.ppermute(block, axis, route)


def from_root(value, axis, root):
    mine = lax.axis_index(axis) == root
    return lax.psum(jnp.where(mine, value, jnp.zeros_like(value)), axis)


def rotate(values_in, positions):
    half_dim = values_in.shape[-1] // 2
    frequency = THETA ** (-jnp.arange(half_dim).astype(jnp.float32) * 2.0 / values_in.shape[-1])
    angles = positions.astype(jnp.float32)[:, None, None] * frequency[None, None, :]
    front_half = values_in[..., :half_dim]
    back_half = values_in[..., half_dim:]
    cosine = jnp.cos(angles)
    sine_part = jnp.sin(angles)
    return jnp.concatenate(
        [front_half * cosine - back_half * sine_part, back_half * cosine + front_half * sine_part],
        axis=-1,
    )


def local(
    hidden_in,
    lengths,
    assign,
    token_ids,
    attn_gain,
    qkv_weight,
    qkv_bias,
    out_weight,
    kv_cache,
    final_gain,
    head_weight,
):
    sections = lax.axis_size("pipe")
    section_index = lax.axis_index("pipe")
    local_count = kv_cache.shape[1]
    query_cols = HEADS * HEAD_DIM
    key_cols = KV_HEADS * HEAD_DIM
    group_size = HEADS // KV_HEADS
    scale_factor = HEAD_DIM ** (-0.5)
    own_ids = lax.axis_index("mp") * local_count + jnp.arange(local_count, dtype=jnp.int32)
    slot_ids = jnp.arange(assign.shape[0], dtype=jnp.int32)
    slot_of = jnp.zeros_like(assign).at[assign].set(slot_ids)
    every_row = slot_of % MB_ROWS
    every_batch = slot_of // MB_ROWS
    own_slots = slot_of[own_ids]
    own_lengths = lengths[own_ids]
    own_rows = own_slots % MB_ROWS
    own_batch = own_slots // MB_ROWS
    visible = jnp.arange(kv_cache.shape[4], dtype=jnp.int32)[None, :] < own_lengths[:, None]
    gain_row = attn_gain[0].astype(jnp.float32)
    weight_in = qkv_weight[0]
    bias_row = qkv_bias[0].astype(jnp.float32)
    weight_out = out_weight[0]
    cache_rows = kv_cache[0]
    slot_table = assign.reshape(MICRO, MB_ROWS)
    row_slots = jnp.arange(MB_ROWS, dtype=jnp.int32)

    def attend_one(request_item):
        queries_one, key_one, value_one, cache_one, visible_one, present_one = request_item

        def compute(unused):
            scores = (
                jnp.einsum(
                    "kgd,kjd->kgj", queries_one, cache_one[0], preferred_element_type=jnp.float32
                )
                * scale_factor
            )
            self_score = (
                jnp.einsum("kgd,kd->kg", queries_one, key_one, preferred_element_type=jnp.float32)
                * scale_factor
            )
            key_mask = visible_one[None, None, :]
            row_top = jnp.maximum(jnp.max(jnp.where(key_mask, scores, -1e30), axis=-1), self_score)
            weights = jnp.where(key_mask, jnp.exp(scores - row_top[..., None]), 0.0)
            self_weight = jnp.exp(self_score - row_top)
            row_total = jnp.sum(weights, axis=-1) + self_weight
            summed = jnp.einsum(
                "kgj,kjd->kgd",
                weights.astype(jnp.bfloat16),
                cache_one[1],
                preferred_element_type=jnp.float32,
            )
            summed = summed + jnp.einsum(
                "kg,kd->kgd",
                self_weight.astype(jnp.bfloat16),
                value_one,
                preferred_element_type=jnp.float32,
            )
            return (summed / row_total[..., None]).astype(jnp.bfloat16).reshape(query_cols)

        def nothing(unused):
            return jnp.zeros((query_cols,), jnp.bfloat16)

        return lax.cond(present_one, compute, nothing, 0)

    def apply_layer(rows_in, batch_index):
        current = rows_in.astype(jnp.float32)
        squares = jnp.sum(current * current, axis=1)
        scaled = (current * gain_row).astype(jnp.bfloat16)
        partial_cols = jnp.dot(scaled, weight_in, preferred_element_type=jnp.float32)
        squares_all = lax.psum(squares, "mp")
        share_cols = lax.psum_scatter(partial_cols, "mp", scatter_dimension=1, tiled=True)
        share_width = share_cols.shape[1]
        share_bias = lax.dynamic_slice_in_dim(
            bias_row, lax.axis_index("mp") * share_width, share_width, 0
        )
        share_cols = share_cols * lax.rsqrt(squares_all / D + EPS)[:, None] + share_bias
        wanted = (
            (every_row[:, None] == row_slots[None, :]) & (every_batch[:, None] == batch_index)
        ).astype(jnp.float32)
        routed_rows = jnp.dot(wanted, share_cols, precision=lax.Precision.HIGHEST)
        picked = lax.all_to_all(routed_rows, "mp", split_axis=0, concat_axis=1, tiled=True)
        queries = rotate(
            picked[:, :query_cols].reshape(local_count, HEADS, HEAD_DIM), own_lengths
        ).astype(jnp.bfloat16)
        queries = queries.reshape(local_count, KV_HEADS, group_size, HEAD_DIM)
        key_new = rotate(
            picked[:, query_cols : query_cols + key_cols].reshape(local_count, KV_HEADS, HEAD_DIM),
            own_lengths,
        ).astype(jnp.bfloat16)
        value_new = (
            picked[:, query_cols + key_cols :]
            .reshape(local_count, KV_HEADS, HEAD_DIM)
            .astype(jnp.bfloat16)
        )
        present = own_batch == batch_index
        attended = lax.map(attend_one, (queries, key_new, value_new, cache_rows, visible, present))
        placing = ((own_rows[:, None] == row_slots[None, :]) & present[:, None]).astype(
            jnp.bfloat16
        )
        spread = jnp.dot(placing.T, attended, preferred_element_type=jnp.float32)
        gathered = lax.psum(spread.astype(jnp.bfloat16), "mp")
        update = jnp.dot(gathered, weight_out, preferred_element_type=jnp.float32)
        return (current + update).astype(jnp.bfloat16)

    def advance(turn_index, state_pair):
        outgoing, finished = state_pair
        incoming = from_behind(outgoing, "pipe", 1)
        offset = turn_index - section_index
        batch_index = jnp.clip(offset, 0, MICRO - 1)
        members = lax.dynamic_index_in_dim(slot_table, batch_index, 0, keepdims=False)
        entering = jnp.take(hidden_in, members, axis=0)
        rows_in = jnp.where(section_index == 0, entering, incoming)
        inside = (offset >= 0) & (offset < MICRO)
        rows_out = apply_layer(rows_in, jnp.where(inside, batch_index, -1))
        storing = inside & (section_index == sections - 1)
        placed = lax.dynamic_update_slice_in_dim(finished, rows_out, batch_index * MB_ROWS, 0)
        return (rows_out, jnp.where(storing, placed, finished))

    outgoing = jnp.zeros((MB_ROWS, hidden_in.shape[1]), jnp.bfloat16)
    finished = jnp.zeros(hidden_in.shape, jnp.bfloat16)
    outgoing, finished = lax.fori_loop(0, MICRO + sections - 1, advance, (outgoing, finished))
    final_rows = from_root(finished, "pipe", sections - 1)
    current = final_rows.astype(jnp.float32)
    squares = lax.psum(jnp.sum(current * current, axis=1), "mp")
    normed = (
        current * final_gain.astype(jnp.float32) * lax.rsqrt(squares / D + EPS)[:, None]
    ).astype(jnp.bfloat16)
    logits = jnp.dot(
        lax.all_gather(normed, "mp", axis=1, tiled=True),
        head_weight,
        preferred_element_type=jnp.float32,
    )
    vocab_width = head_weight.shape[1]
    vocab_ids = lax.axis_index(("pipe", "mp")) * vocab_width + jnp.arange(
        vocab_width, dtype=jnp.int32
    )
    targets = token_ids[assign]
    matches = vocab_ids[None, :] == targets[:, None]
    picked_local = jnp.sum(jnp.where(matches, logits, 0.0), axis=1)
    local_top = jnp.max(logits, axis=1)
    row_top = lax.pmax(local_top, ("pipe", "mp"))
    local_total = jnp.sum(jnp.exp(logits - row_top[:, None]), axis=1)
    row_total, picked = lax.psum((local_total, picked_local), ("pipe", "mp"))
    log_total = row_top + jnp.log(row_total)
    return (logits - log_total[:, None], picked - log_total)


def solution(mesh):
    return jax.shard_map(
        local,
        mesh=mesh,
        in_specs=(
            P(None, "mp"),
            P(),
            P(),
            P(),
            P("pipe", "mp"),
            P("pipe", "mp", None),
            P("pipe", None),
            P("pipe", None, "mp"),
            P("pipe", "mp", None, None, None, None),
            P("mp"),
            P(None, ("pipe", "mp")),
        ),
        out_specs=(P(None, ("pipe", "mp")), P()),
        check_vma=False,
    )
```

profile of v0, /device:TPU:0, one launch (start us, length us, event | category | flops | bytes accessed | tf_op | source)
XLA Modules:
  0.0 1342.7 jit_solution(10831050884700243807)
XLA Ops:
  13.6 1149.9 %while.53 = (s32[]{:T(128)}, bf16[8,1024]{1,0:T(8,128)(2,1)S(1)}, bf16[32,1024]{1,0:T(8,128)(2,1)S(1)}, pred[]{:T(512)}, s32[]{:T(128)}, /*index=5*/s32[4,8]{1,0...) while((s32[]{:T(128)}, bf16[8,1024]{1,0:T(8,128)(2,1)S(1)}, ...), condition=%wide.region_12.13_spmd.clone.clone, body=%wide.region_1.12_spmd.clone.clone.sunk | while | flops 157849424 | bytes 22136348 | solution.py:175
  18.0 6.1 fusion.85
  24.2 22.5 %psum.66 = f32[8]{0:T(128)S(1)} all-reduce(f32[8]{0:T(128)S(1)} %get-tuple-element.929), channel_id=1, replica_groups=mesh['pipe'=4,'mp'=8] {'mp'}, use_global_device_ids=true, to_apply=%region_4.4 | all-reduce | flops 8 | bytes 64 | tf_op jit(solution)/shard_map/while/body/eval_jaxpr/psum | solution.py:124
  46.7 36.4 %reduce-scatter.2.cloned.1.call-done = f32[8,640]{1,0:T(8,128)} async-done(((f32[8,5120]{1,0:T(8,128)}), f32[8,640]{1,0:T(8,128)}) %reduce-scatter.2.cloned.1.call-update) | async-done | bytes 20496 | tf_op jit(solution)/shard_map/while/body/eval_jaxpr/reduce_scatter | solution.py:125
  88.4 7.0 all-to-all-done
  95.8 11.8 while.54
  108.5 65.4 %all-reduce.6.cloned.1.call-done = bf16[8,4096]{1,0:T(8,128)(2,1)} async-done(((bf16[8,4096]{1,0:T(8,128)(2,1)}), bf16[8,4096]{1,0:T(8,128)(2,1)}) %all-reduce.6.cloned.1.call-update) | async-done | bytes 65552 | tf_op jit(solution)/shard_map/while/body/eval_jaxpr/psum | solution.py:155
  181.8 6.1 fusion.85
  188.0 20.4 %psum.66 = f32[8]{0:T(128)S(1)} all-reduce(f32[8]{0:T(128)S(1)} %get-tuple-element.929), channel_id=1, replica_groups=mesh['pipe'=4,'mp'=8] {'mp'}, use_global_device_ids=true, to_apply=%region_4.4 | all-reduce | flops 8 | bytes 64 | tf_op jit(solution)/shard_map/while/body/eval_jaxpr/psum | solution.py:124
  208.4 36.8 %reduce-scatter.2.cloned.1.call-done = f32[8,640]{1,0:T(8,128)} async-done(((f32[8,5120]{1,0:T(8,128)}), f32[8,640]{1,0:T(8,128)}) %reduce-scatter.2.cloned.1.call-update) | async-done | bytes 20496 | tf_op jit(solution)/shard_map/while/body/eval_jaxpr/reduce_scatter | solution.py:125
  250.5 7.0 all-to-all-done
  257.9 9.1 while.54
  267.9 71.3 %all-reduce.6.cloned.1.call-done = bf16[8,4096]{1,0:T(8,128)(2,1)} async-done(((bf16[8,4096]{1,0:T(8,128)(2,1)}), bf16[8,4096]{1,0:T(8,128)(2,1)}) %all-reduce.6.cloned.1.call-update) | async-done | bytes 65552 | tf_op jit(solution)/shard_map/while/body/eval_jaxpr/psum | solution.py:155
  347.0 6.1 fusion.85
  353.3 20.4 %psum.66 = f32[8]{0:T(128)S(1)} all-reduce(f32[8]{0:T(128)S(1)} %get-tuple-element.929), channel_id=1, replica_groups=mesh['pipe'=4,'mp'=8] {'mp'}, use_global_device_ids=true, to_apply=%region_4.4 | all-reduce | flops 8 | bytes 64 | tf_op jit(solution)/shard_map/while/body/eval_jaxpr/psum | solution.py:124
  373.7 36.8 %reduce-scatter.2.cloned.1.call-done = f32[8,640]{1,0:T(8,128)} async-done(((f32[8,5120]{1,0:T(8,128)}), f32[8,640]{1,0:T(8,128)}) %reduce-scatter.2.cloned.1.call-update) | async-done | bytes 20496 | tf_op jit(solution)/shard_map/while/body/eval_jaxpr/reduce_scatter | solution.py:125
  415.8 7.0 all-to-all-done
  423.1 6.4 while.54
  430.4 73.9 %all-reduce.6.cloned.1.call-done = bf16[8,4096]{1,0:T(8,128)(2,1)} async-done(((bf16[8,4096]{1,0:T(8,128)(2,1)}), bf16[8,4096]{1,0:T(8,128)(2,1)}) %all-reduce.6.cloned.1.call-update) | async-done | bytes 65552 | tf_op jit(solution)/shard_map/while/body/eval_jaxpr/psum | solution.py:155
  512.2 6.1 fusion.85
  518.5 20.4 %psum.66 = f32[8]{0:T(128)S(1)} all-reduce(f32[8]{0:T(128)S(1)} %get-tuple-element.929), channel_id=1, replica_groups=mesh['pipe'=4,'mp'=8] {'mp'}, use_global_device_ids=true, to_apply=%region_4.4 | all-reduce | flops 8 | bytes 64 | tf_op jit(solution)/shard_map/while/body/eval_jaxpr/psum | solution.py:124
  538.8 36.8 %reduce-scatter.2.cloned.1.call-done = f32[8,640]{1,0:T(8,128)} async-done(((f32[8,5120]{1,0:T(8,128)}), f32[8,640]{1,0:T(8,128)}) %reduce-scatter.2.cloned.1.call-update) | async-done | bytes 20496 | tf_op jit(solution)/shard_map/while/body/eval_jaxpr/reduce_scatter | solution.py:125
  581.0 7.0 all-to-all-done
  588.3 9.1 while.54
  598.4 72.2 %all-reduce.6.cloned.1.call-done = bf16[8,4096]{1,0:T(8,128)(2,1)} async-done(((bf16[8,4096]{1,0:T(8,128)(2,1)}), bf16[8,4096]{1,0:T(8,128)(2,1)}) %all-reduce.6.cloned.1.call-update) | async-done | bytes 65552 | tf_op jit(solution)/shard_map/while/body/eval_jaxpr/psum | solution.py:155
  678.4 6.1 fusion.85
  684.7 20.4 %psum.66 = f32[8]{0:T(128)S(1)} all-reduce(f32[8]{0:T(128)S(1)} %get-tuple-element.929), channel_id=1, replica_groups=mesh['pipe'=4,'mp'=8] {'mp'}, use_global_device_ids=true, to_apply=%region_4.4 | all-reduce | flops 8 | bytes 64 | tf_op jit(solution)/shard_map/while/body/eval_jaxpr/psum | solution.py:124
  705.0 36.8 %reduce-scatter.2.cloned.1.call-done = f32[8,640]{1,0:T(8,128)} async-done(((f32[8,5120]{1,0:T(8,128)}), f32[8,640]{1,0:T(8,128)}) %reduce-scatter.2.cloned.1.call-update) | async-done | bytes 20496 | tf_op jit(solution)/shard_map/while/body/eval_jaxpr/reduce_scatter | solution.py:125
  747.2 7.0 all-to-all-done
  754.5 6.4 while.54
  761.8 74.8 %all-reduce.6.cloned.1.call-done = bf16[8,4096]{1,0:T(8,128)(2,1)} async-done(((bf16[8,4096]{1,0:T(8,128)(2,1)}), bf16[8,4096]{1,0:T(8,128)(2,1)}) %all-reduce.6.cloned.1.call-update) | async-done | bytes 65552 | tf_op jit(solution)/shard_map/while/body/eval_jaxpr/psum | solution.py:155
  844.5 6.1 fusion.85
  850.7 20.4 %psum.66 = f32[8]{0:T(128)S(1)} all-reduce(f32[8]{0:T(128)S(1)} %get-tuple-element.929), channel_id=1, replica_groups=mesh['pipe'=4,'mp'=8] {'mp'}, use_global_device_ids=true, to_apply=%region_4.4 | all-reduce | flops 8 | bytes 64 | tf_op jit(solution)/shard_map/while/body/eval_jaxpr/psum | solution.py:124
  871.1 36.8 %reduce-scatter.2.cloned.1.call-done = f32[8,640]{1,0:T(8,128)} async-done(((f32[8,5120]{1,0:T(8,128)}), f32[8,640]{1,0:T(8,128)}) %reduce-scatter.2.cloned.1.call-update) | async-done | bytes 20496 | tf_op jit(solution)/shard_map/while/body/eval_jaxpr/reduce_scatter | solution.py:125
  913.2 7.0 all-to-all-done
  920.6 6.4 while.54
  927.9 71.9 %all-reduce.6.cloned.1.call-done = bf16[8,4096]{1,0:T(8,128)(2,1)} async-done(((bf16[8,4096]{1,0:T(8,128)(2,1)}), bf16[8,4096]{1,0:T(8,128)(2,1)}) %all-reduce.6.cloned.1.call-update) | async-done | bytes 65552 | tf_op jit(solution)/shard_map/while/body/eval_jaxpr/psum | solution.py:155
  1007.6 6.1 fusion.85
  1013.8 20.4 %psum.66 = f32[8]{0:T(128)S(1)} all-reduce(f32[8]{0:T(128)S(1)} %get-tuple-element.929), channel_id=1, replica_groups=mesh['pipe'=4,'mp'=8] {'mp'}, use_global_device_ids=true, to_apply=%region_4.4 | all-reduce | flops 8 | bytes 64 | tf_op jit(solution)/shard_map/while/body/eval_jaxpr/psum | solution.py:124
  1034.2 36.8 %reduce-scatter.2.cloned.1.call-done = f32[8,640]{1,0:T(8,128)} async-done(((f32[8,5120]{1,0:T(8,128)}), f32[8,640]{1,0:T(8,128)}) %reduce-scatter.2.cloned.1.call-update) | async-done | bytes 20496 | tf_op jit(solution)/shard_map/while/body/eval_jaxpr/reduce_scatter | solution.py:125
  1076.3 7.0 all-to-all-done
  1083.7 6.4 while.54
  1091.0 67.9 %all-reduce.6.cloned.1.call-done = bf16[8,4096]{1,0:T(8,128)(2,1)} async-done(((bf16[8,4096]{1,0:T(8,128)(2,1)}), bf16[8,4096]{1,0:T(8,128)(2,1)}) %all-reduce.6.cloned.1.call-update) | async-done | bytes 65552 | tf_op jit(solution)/shard_map/while/body/eval_jaxpr/psum | solution.py:155
  1164.9 32.6 %all-reduce.4.cloned.1.call-done = bf16[32,1024]{1,0:T(8,128)(2,1)} async-done(((bf16[32,1024]{1,0:T(8,128)(2,1)}), bf16[32,1024]{1,0:T(8,128)(2,1)}) %all-reduce.4.cloned.1.call-update) | async-done | bytes 65552 | tf_op jit(solution)/shard_map/psum | solution.py:26
  1198.5 21.4 %psum.57 = f32[32]{0:T(128)S(1)} all-reduce(f32[32]{0:T(128)S(1)} %fusion.50), channel_id=1, replica_groups=mesh['pipe'=4,'mp'=8] {'mp'}, use_global_device_ids=true, to_apply=%region_15.16 | all-reduce | flops 32 | bytes 256 | tf_op jit(solution)/shard_map/psum | solution.py:178
  1220.8 31.4 %all_gather.3 = bf16[32,8192]{1,0:T(8,128)(2,1)S(1)} all-gather(bf16[32,1024]{1,0:T(8,128)(2,1)S(1)} %fusion.49), channel_id=1, replica_groups=mesh['pipe'=4,'mp'=8] {'mp'}, dimensions={1}, use_global_device_ids=true | all-gather | bytes 589824 | tf_op jit(solution)/shard_map/all_gather | solution.py:183
  1256.1 36.8 %pmax.7 = f32[32]{0:T(128)S(1)} all-reduce(f32[32]{0:T(128)S(1)} %get-tuple-element.743), channel_id=1, replica_groups=mesh['pipe'=4,'mp'=8] {'pipe','mp'}, use_global_device_ids=true, to_apply=%region_17.18 | all-reduce | flops 32 | bytes 256 | tf_op jit(solution)/shard_map/pmax | solution.py:195
  1293.2 41.2 %all-reduce = (f32[32]{0:T(128)S(1)}, f32[32]{0:T(128)S(1)}) all-reduce(f32[32]{0:T(128)S(1)} %get-tuple-element.666, f32[32]{0:T(128)S(1)} %get-tuple-element.665), channel_id=1, replica_groups=mesh['pipe'=4,'mp'=8] {'pipe','mp'}, use_global_device_ids=true, to_apply=%region_19.20 | all-reduce | flops 64 | bytes 512 | tf_op jit(solution)/shard_map/psum | solution.py:197
  (426 shorter events, 162.7 us)
Async XLA Ops:
  8.0 1156.2 %copy-start = (s32[32]{0:T(128)S(1)}, s32[32]{0:T(128)}, u32[]{:S(2)}) copy-start(s32[32]{0:T(128)} %param.20) | copy-start | bytes 388
  13.6 1150.6 %copy-start.1 = (bf16[1024]{0:T(1024)(128)(2,1)S(1)}, bf16[1024]{0:T(1024)(128)(2,1)}, u32[]{:S(2)}) copy-start(bf16[1024]{0:T(1024)(128)(2,1)} %param.26) | copy-start | bytes 6148
  13.6 69.5 %reduce-scatter.2.cloned.1.call-start = ((), (), s32[]{:S(2)}) async-start(), calls=%async_computation.3 | async-start | bytes 184320 | tf_op jit(solution)/shard_map/while/body/eval_jaxpr/reduce_scatter | solution.py:125
  13.7 4.1 collective-permute-start
  84.7 10.6 all-to-all-start
  88.3 85.6 %all-reduce.6.cloned.1.call-start = ((), (), s32[]{:S(2)}) async-start(), calls=%async_computation.4 | async-start | bytes 131072 | tf_op jit(solution)/shard_map/while/body/eval_jaxpr/psum | solution.py:155
  178.5 66.7 %reduce-scatter.2.cloned.1.call-start = ((), (), s32[]{:S(2)}) async-start(), calls=%async_computation.3 | async-start | bytes 184320 | tf_op jit(solution)/shard_map/while/body/eval_jaxpr/reduce_scatter | solution.py:125
  178.6 3.0 collective-permute-start
  246.8 10.6 all-to-all-start
  250.4 88.8 %all-reduce.6.cloned.1.call-start = ((), (), s32[]{:S(2)}) async-start(), calls=%async_computation.4 | async-start | bytes 131072 | tf_op jit(solution)/shard_map/while/body/eval_jaxpr/psum | solution.py:155
  343.8 66.7 %reduce-scatter.2.cloned.1.call-start = ((), (), s32[]{:S(2)}) async-start(), calls=%async_computation.3 | async-start | bytes 184320 | tf_op jit(solution)/shard_map/while/body/eval_jaxpr/reduce_scatter | solution.py:125
  343.8 3.0 collective-permute-start
  412.1 10.6 all-to-all-start
  415.7 88.7 %all-reduce.6.cloned.1.call-start = ((), (), s32[]{:S(2)}) async-start(), calls=%async_computation.4 | async-start | bytes 131072 | tf_op jit(solution)/shard_map/while/body/eval_jaxpr/psum | solution.py:155
  509.0 66.7 %reduce-scatter.2.cloned.1.call-start = ((), (), s32[]{:S(2)}) async-start(), calls=%async_computation.3 | async-start | bytes 184320 | tf_op jit(solution)/shard_map/while/body/eval_jaxpr/reduce_scatter | solution.py:125
  509.0 3.0 collective-permute-start
  577.3 10.6 all-to-all-start
  580.9 89.7 %all-reduce.6.cloned.1.call-start = ((), (), s32[]{:S(2)}) async-start(), calls=%async_computation.4 | async-start | bytes 131072 | tf_op jit(solution)/shard_map/while/body/eval_jaxpr/psum | solution.py:155
  675.2 66.7 %reduce-scatter.2.cloned.1.call-start = ((), (), s32[]{:S(2)}) async-start(), calls=%async_computation.3 | async-start | bytes 184320 | tf_op jit(solution)/shard_map/while/body/eval_jaxpr/reduce_scatter | solution.py:125
  675.2 3.0 collective-permute-start
  743.5 10.6 all-to-all-start
  747.1 89.6 %all-reduce.6.cloned.1.call-start = ((), (), s32[]{:S(2)}) async-start(), calls=%async_computation.4 | async-start | bytes 131072 | tf_op jit(solution)/shard_map/while/body/eval_jaxpr/psum | solution.py:155
  841.3 66.7 %reduce-scatter.2.cloned.1.call-start = ((), (), s32[]{:S(2)}) async-start(), calls=%async_computation.3 | async-start | bytes 184320 | tf_op jit(solution)/shard_map/while/body/eval_jaxpr/reduce_scatter | solution.py:125
  841.3 3.0 collective-permute-start
  909.6 10.6 all-to-all-start
  913.2 86.6 %all-reduce.6.cloned.1.call-start = ((), (), s32[]{:S(2)}) async-start(), calls=%async_computation.4 | async-start | bytes 131072 | tf_op jit(solution)/shard_map/while/body/eval_jaxpr/psum | solution.py:155
  1004.4 66.7 %reduce-scatter.2.cloned.1.call-start = ((), (), s32[]{:S(2)}) async-start(), calls=%async_computation.3 | async-start | bytes 184320 | tf_op jit(solution)/shard_map/while/body/eval_jaxpr/reduce_scatter | solution.py:125
  1004.4 3.0 collective-permute-start
  1072.7 10.6 all-to-all-start
  1076.3 82.6 %all-reduce.6.cloned.1.call-start = ((), (), s32[]{:S(2)}) async-start(), calls=%async_computation.4 | async-start | bytes 131072 | tf_op jit(solution)/shard_map/while/body/eval_jaxpr/psum | solution.py:155
  1163.5 34.1 %all-reduce.4.cloned.1.call-start = ((), (), s32[]{:S(2)}) async-start(), calls=%async_computation.2 | async-start | bytes 131072 | tf_op jit(solution)/shard_map/psum | solution.py:26
Sparse Core Ops, SparseCore 0:
  24.2 58.8 reduce-scatter.1
  108.6 65.2 all-reduce.5
  188.0 57.1 reduce-scatter.1
  268.0 71.1 all-reduce.5
  353.3 57.1 reduce-scatter.1
  430.6 73.7 all-reduce.5
  518.5 57.1 reduce-scatter.1
  598.5 72.0 all-reduce.5
  684.7 57.1 reduce-scatter.1
  761.9 74.6 all-reduce.5
  850.8 57.1 reduce-scatter.1
  928.0 71.6 all-reduce.5
  1013.9 57.1 reduce-scatter.1
  1091.1 67.7 all-reduce.5
Sparse Core Ops, SparseCore 1:
  1166.3 31.2 all-reduce.3
where the time goes:
time: 1340 us
  waiting for transfers between devices  836 us (62%)
  blocking collectives  276 us (21%)
  matrix products  102 us (8%)
  local copies, waits for them, and re-layouts  43.2 us (3%)
  starting transfers between devices  35.9 us (3%)
  loops' own time  22.4 us (2%)
  between operations  15.3 us (1%)
    psum x7, waiting for transfers between devices, apply_layer(): gathered = lax.psum(spread.astype(jnp.bfloat16), 'mp')  497 us
    reduce_scatter x7, waiting for transfers between devices, apply_layer(): lax.psum_scatter(partial_cols, 'mp', scatter_dimension=1, tiled=True)  257 us
    psum x7, blocking collectives, apply_layer(): squares_all = lax.psum(squares, 'mp')  145 us
    all_to_all x7, waiting for transfers between devices, apply_layer(): lax.all_to_all(routed_rows, 'mp', split_axis=0, concat_axis=1, tiled=True)  48.7 us
    dot_general x7, matrix products, apply_layer(): jnp.dot(scaled, weight_in, preferred_element_type=jnp.float32)  42.7 us
    psum x1, blocking collectives, local(): row_total, picked = lax.psum((local_total, picked_local), ('pipe', 'mp'))  41.2 us
    pmax x1, blocking collectives, local(): row_top = lax.pmax(local_top, ('pipe', 'mp'))  36.8 us
    psum x1, waiting for transfers between devices, from_root(): return lax.psum(jnp.where(mine, value, jnp.zeros_like(value)), axis)  32.6 us
  transfers between devices with their start and end apart: 29, of which 22 were waited for; matrix products, arithmetic and copies ran while one was open for 1% of the time, Pallas kernels for 0%

commit v1 on v0

v1 whole, which is shorter than its diff:
```python
import functools

import jax
import jax.numpy as jnp
import numpy as np
from jax import lax
from jax.experimental import pallas as pl
from jax.experimental.pallas import tpu as pltpu
from jax.sharding import PartitionSpec as P

HEADS = 32
KV_HEADS = 4
HEAD_DIM = 128
EPS = 1e-06
THETA = 1000000.0
MESH = pl.DeviceIdType.MESH
F32 = jnp.float32
BF16 = jnp.bfloat16


def remote(src, dst, send_sem, recv_sem, device):
    return pltpu.make_async_remote_copy(
        src_ref=src,
        dst_ref=dst,
        send_sem=send_sem,
        recv_sem=recv_sem,
        device_id=device,
        device_id_type=MESH,
    )


def kernel(
    sections,
    n,
    hidden,
    lengths,
    assign,
    token_ids,
    gain,
    qkv_weight,
    bias,
    out_weight,
    cache,
    final_gain,
    head_weight,
    freq,
    out,
    chosen,
    wq,
    wo,
    kv,
    hw,
    x,
    xo,
    scaled,
    part,
    part_in,
    sq,
    sq_in,
    bias_rows,
    att,
    att_in,
    att_rows,
    att_mat,
    fin,
    fsq,
    fsq_in,
    red,
    red_in,
    wq_sem,
    w_sem,
    part_s,
    part_r,
    sq_s,
    sq_r,
    att_s,
    att_r,
    hop_s,
    hop_r,
    fin_s,
    fin_r,
    fsq_s,
    fsq_r,
    fp_s,
    fp_r,
    red_s,
    red_r,
):
    sec = lax.axis_index("pipe")
    me = lax.axis_index("mp")
    total = sections * n
    rows, width = hidden.shape
    lc = kv.shape[0]
    heads_all = HEADS + 2 * KV_HEADS
    group = HEADS // KV_HEADS
    last = sections - 1
    scale = HEAD_DIM ** (-0.5)
    chunks = wq_sem.shape[0]
    cw = wq.shape[1] // chunks

    def wq_copy(c):
        cols = pl.ds(pl.multiple_of(c * cw, cw), cw)
        return pltpu.make_async_copy(qkv_weight.at[0, :, cols], wq.at[:, cols], wq_sem.at[c])

    for c in range(chunks):
        wq_copy(c).start()
    kv_copy = pltpu.make_async_copy(cache.at[0], kv, w_sem.at[0])
    wo_copy = pltpu.make_async_copy(out_weight.at[0], wo, w_sem.at[1])
    hw_copy = pltpu.make_async_copy(head_weight, hw, w_sem.at[2])
    kv_copy.start()
    wo_copy.start()
    hw_copy.start()

    barrier = pltpu.get_barrier_semaphore()
    mine = sec * n + me

    def greet(k, carry):
        other = lax.rem(mine + k, total)
        pl.semaphore_signal(
            barrier, inc=1, device_id=(other // n, lax.rem(other, n)), device_id_type=MESH
        )
        return carry

    lax.fori_loop(1, total, greet, 0)

    for i in range(heads_all):
        bias_rows[i : i + 1, :] = bias[:, i * HEAD_DIM : (i + 1) * HEAD_DIM].astype(F32)
    eye = lax.broadcasted_iota(jnp.int32, (rows, 128), 0) == lax.broadcasted_iota(
        jnp.int32, (rows, 128), 1
    )

    def to_row(col):
        return jnp.sum(jnp.where(eye, col, 0.0), axis=0, keepdims=True)

    def to_col(row):
        return jnp.sum(jnp.where(eye, row, 0.0), axis=1, keepdims=True)

    small_eye = lax.broadcasted_iota(jnp.int32, (rows, rows), 0) == lax.broadcasted_iota(
        jnp.int32, (rows, rows), 1
    )
    assign_col = jnp.sum(
        jnp.where(small_eye, assign[...].astype(F32), 0.0), axis=1, keepdims=True
    )
    order = assign_col == lax.broadcasted_iota(jnp.int32, (rows, rows), 1).astype(F32)
    target = jnp.sum(
        jnp.where(order, token_ids[...].astype(F32), 0.0), axis=1, keepdims=True
    )
    lane = lax.broadcasted_iota(jnp.int32, (1, HEAD_DIM), 1)
    lane_rows = lax.broadcasted_iota(jnp.int32, (1, rows), 1)
    own_len = [
        jnp.sum(
            jnp.where(lane_rows == me * lc + i, lengths[...].astype(F32), 0.0),
            axis=1,
            keepdims=True,
        )
        for i in range(lc)
    ]
    angles = jnp.concatenate([length * freq[...] for length in own_len], axis=0)
    cosine = jnp.cos(angles)
    sine = jnp.sin(angles) * jnp.where(lane < HEAD_DIM // 2, -1.0, 1.0)

    pl.semaphore_wait(barrier, total - 1)

    @pl.when(sec == 0)
    def _():
        x[...] = hidden[...]

    @pl.when(sec > 0)
    def _():
        remote(xo, x, hop_s, hop_r, (sec - 1, me)).wait_recv()

    current = x[...].astype(F32)
    sq[...] = jnp.broadcast_to(
        to_row(jnp.sum(current * current, axis=1, keepdims=True)), sq.shape
    )
    scaled[...] = (current * gain[...].astype(F32)).astype(BF16)

    def sq_copy(peer, slot, sem):
        return remote(sq, sq_in.at[slot], sq_s.at[peer], sq_r.at[sem], (sec, peer))

    for k in range(1, n):
        peer = lax.rem(me + k, n)
        sq_copy(peer, me, me).start()

    per = cw // HEAD_DIM

    def project(c, carry):
        wq_copy(c).wait()
        cols = pl.ds(pl.multiple_of(c * cw, cw), cw)
        piece = jnp.dot(scaled[...], wq[:, cols], preferred_element_type=F32)
        for j in range(per):
            part[pl.ds(c * per + j, rows, stride=heads_all), :] = piece[
                :, j * HEAD_DIM : (j + 1) * HEAD_DIM
            ]
        return carry

    lax.fori_loop(0, chunks, project, 0)

    block = lc * heads_all

    def part_copy(peer, slot):
        return remote(
            part.at[pl.ds(pl.multiple_of(peer * block, block), block), :],
            part_in.at[slot],
            part_s.at[peer],
            part_r.at[slot],
            (sec, peer),
        )

    for k in range(1, n):
        part_copy(lax.rem(me + k, n), me).start()

    squares = sq[...]
    for k in range(1, n):
        peer = lax.rem(me + n - k, n)
        sq_copy(peer, peer, peer).wait_recv()
        squares = squares + sq_in[peer]
    summed_cols = part[pl.ds(pl.multiple_of(me * block, block), block), :]
    for k in range(1, n):
        peer = lax.rem(me + n - k, n)
        part_copy(peer, peer).wait_recv()
        summed_cols = summed_cols + part_in[peer]
    kv_copy.wait()
    pos = lax.broadcasted_iota(jnp.int32, (1, kv.shape[3]), 1).astype(F32)
    for i in range(lc):
        mean = (
            jnp.sum(
                jnp.where(lane == me * lc + i, squares[0:1, :], 0.0), axis=1, keepdims=True
            )
            / (n * width)
        )
        rows_i = summed_cols[i * heads_all : (i + 1) * heads_all] * lax.rsqrt(
            mean + EPS
        ) + bias_rows[...]
        turned = (
            rows_i * cosine[i : i + 1]
            + pltpu.roll(rows_i, HEAD_DIM // 2, 1) * sine[i : i + 1]
        )
        visible = pos < own_len[i]
        heads = []
        for h in range(KV_HEADS):
            query = turned[h * group : (h + 1) * group].astype(BF16)
            key_new = turned[HEADS + h : HEADS + h + 1].astype(BF16).astype(F32)
            at = HEADS + KV_HEADS + h
            value_new = rows_i[at : at + 1].astype(BF16).astype(F32)
            scores = (
                lax.dot_general(
                    query,
                    kv[i, 0, h],
                    (((1,), (1,)), ((), ())),
                    preferred_element_type=F32,
                )
                * scale
            )
            self_score = (
                jnp.sum(query.astype(F32) * key_new, axis=1, keepdims=True) * scale
            )
            top = jnp.maximum(
                jnp.max(jnp.where(visible, scores, -1e30), axis=1, keepdims=True), self_score
            )
            weights = jnp.where(visible, jnp.exp(scores - top), 0.0)
            self_weight = jnp.exp(self_score - top)
            denominator = jnp.sum(weights, axis=1, keepdims=True) + self_weight
            mixed = jnp.dot(weights.astype(BF16), kv[i, 1, h], preferred_element_type=F32)
            mixed = mixed + self_weight.astype(BF16).astype(F32) * value_new
            heads.append(mixed / denominator)
        att[i * HEADS : (i + 1) * HEADS, :] = jnp.concatenate(heads, axis=0).astype(BF16)

    def att_copy(peer, slot):
        return remote(att, att_in.at[slot], att_s.at[peer], att_r.at[slot], (sec, peer))

    for k in range(1, n):
        att_copy(lax.rem(me + k, n), me).start()
    span = lc * HEADS
    att_rows[pl.ds(pl.multiple_of(me * span, span), span), :] = att[...].astype(F32)
    for k in range(1, n):
        peer = lax.rem(me + n - k, n)
        att_copy(peer, peer).wait_recv()
        att_rows[pl.ds(pl.multiple_of(peer * span, span), span), :] = att_in[peer].astype(F32)
    for i in range(HEADS):
        att_mat[:, i * HEAD_DIM : (i + 1) * HEAD_DIM] = att_rows[
            pl.ds(i, rows, stride=HEADS), :
        ].astype(BF16)
    wo_copy.wait()
    ow = min(256, width)

    def project_out(c, carry):
        cols = pl.ds(pl.multiple_of(c * ow, ow), ow)
        update = jnp.dot(att_mat[...], wo[:, cols], preferred_element_type=F32)
        xo[:, cols] = (x[:, cols].astype(F32) + update).astype(BF16)
        return carry

    lax.fori_loop(0, width // ow, project_out, 0)

    @pl.when(sec < last)
    def _():
        hop = remote(xo, x, hop_s, hop_r, (sec + 1, me))
        hop.start()
        hop.wait_send()

    def fin_pipe(k, from_here):
        to = lax.rem(sec + k, sections)
        dev = (to, me)
        return (
            remote(fin.at[me], fin.at[me], fp_s.at[2 * k], fp_r.at[0], dev),
            remote(fsq_in.at[me], fsq_in.at[me], fp_s.at[2 * k + 1], fp_r.at[1], dev),
        )

    @pl.when(sec == last)
    def _():
        final = jnp.dot(order.astype(BF16), xo[...], preferred_element_type=F32)
        fin[me] = (final * final_gain[...].astype(F32)).astype(BF16)
        fsq_in[me] = jnp.broadcast_to(
            to_row(jnp.sum(final * final, axis=1, keepdims=True)), fsq.shape
        )
        for k in range(1, sections):
            for copy in fin_pipe(k, True):
                copy.start()

    @pl.when(sec < last)
    def _():
        for copy in fin_pipe(1, False):
            copy.wait_recv()

    def fin_copy(peer, slot):
        return remote(
            fin.at[slot], fin.at[slot], fin_s.at[peer], fin_r.at[slot], (sec, peer)
        )

    def fsq_copy(peer, slot):
        return remote(
            fsq_in.at[slot], fsq_in.at[slot], fsq_s.at[peer], fsq_r.at[slot], (sec, peer)
        )

    for k in range(1, n):
        peer = lax.rem(me + k, n)
        fin_copy(peer, me).start()
        fsq_copy(peer, me).start()
    hw_copy.wait()

    def head(k, logits):
        peer = lax.rem(me + n - k, n)

        @pl.when(k > 0)
        def _():
            fin_copy(peer, peer).wait_recv()

        rows_at = pl.ds(pl.multiple_of(peer * width, width), width)
        return logits + jnp.dot(fin[peer], hw[rows_at, :], preferred_element_type=F32)

    logits = lax.fori_loop(0, n, head, jnp.zeros(out.shape, F32))
    squares = fsq_in[me]
    for k in range(1, n):
        peer = lax.rem(me + n - k, n)
        fsq_copy(peer, peer).wait_recv()
        squares = squares + fsq_in[peer]
    logits = logits * lax.rsqrt(to_col(squares[0:1, :]) / (n * width) + EPS)
    vocab = out.shape[1]
    ids = (mine * vocab + lax.broadcasted_iota(jnp.int32, (1, vocab), 1)).astype(F32)
    picked = jnp.sum(jnp.where(ids == target, logits, 0.0), axis=1, keepdims=True)
    top = jnp.max(logits, axis=1, keepdims=True)
    amount = jnp.sum(jnp.exp(logits - top), axis=1, keepdims=True)
    red[...] = jnp.concatenate(
        [to_row(top), to_row(amount), to_row(picked), jnp.zeros((5, 128), F32)], axis=0
    )

    def red_copy(other, slot):
        return remote(
            red,
            red_in.at[slot],
            red_s.at[other],
            red_r.at[slot],
            (other // n, lax.rem(other, n)),
        )

    def red_start(k, carry):
        red_copy(lax.rem(mine + k, total), mine).start()
        return carry

    lax.fori_loop(1, total, red_start, 0)
    red_in[mine] = red[...]

    def red_wait(k, carry):
        other = lax.rem(mine + total - k, total)
        red_copy(other, other).wait_recv()
        return carry

    lax.fori_loop(1, total, red_wait, 0)
    tops = red_in[:, 0, :]
    row_top = jnp.max(tops, axis=0, keepdims=True)
    row_total = jnp.sum(red_in[:, 1, :] * jnp.exp(tops - row_top), axis=0, keepdims=True)
    log_total = row_top + jnp.log(row_total)
    chosen[...] = jnp.sum(red_in[:, 2, :], axis=0, keepdims=True) - log_total
    out[...] = logits - to_col(log_total)

    for k in range(1, n):
        peer = lax.rem(me + k, n)
        sq_copy(peer, me, me).wait_send()
        part_copy(peer, me).wait_send()
        att_copy(peer, me).wait_send()
        fin_copy(peer, me).wait_send()
        fsq_copy(peer, me).wait_send()

    @pl.when(sec == last)
    def _():
        for k in range(1, sections):
            for copy in fin_pipe(k, True):
                copy.wait_send()

    def red_done(k, carry):
        red_copy(lax.rem(mine + k, total), mine).wait_send()
        return carry

    lax.fori_loop(1, total, red_done, 0)


def local(
    hidden_in,
    lengths,
    assign,
    token_ids,
    attn_gain,
    qkv_weight,
    qkv_bias,
    out_weight,
    kv_cache,
    final_gain,
    head_weight,
):
    sections = lax.axis_size("pipe")
    n = lax.axis_size("mp")
    rows, width = hidden_in.shape
    lc = kv_cache.shape[1]
    qkv = qkv_weight.shape[2]
    inner = out_weight.shape[1]
    vocab = head_weight.shape[1]
    heads_all = HEADS + 2 * KV_HEADS
    half = HEAD_DIM // 2
    frequency = np.float32(THETA) ** (
        -np.arange(half).astype(np.float32) * np.float32(2.0) / np.float32(HEAD_DIM)
    )
    freq = jnp.asarray(np.concatenate([frequency, frequency])[None, :], F32)
    chunks = qkv // 512
    dma = pltpu.SemaphoreType.DMA
    vm = pl.BlockSpec(memory_space=pltpu.VMEM)
    hbm = pl.BlockSpec(memory_space=pl.ANY)
    total = sections * n
    logprobs, chosen = pl.pallas_call(
        functools.partial(kernel, sections, n),
        out_shape=(
            jax.ShapeDtypeStruct((rows, vocab), F32),
            jax.ShapeDtypeStruct((1, 128), F32),
        ),
        in_specs=[vm, vm, vm, vm, vm, hbm, vm, hbm, hbm, vm, hbm, vm],
        out_specs=(vm, vm),
        scratch_shapes=[
            pltpu.VMEM((width, qkv), BF16),
            pltpu.VMEM((inner, width), BF16),
            pltpu.VMEM(kv_cache.shape[1:], BF16),
            pltpu.VMEM(head_weight.shape, BF16),
            pltpu.VMEM((rows, width), BF16),
            pltpu.VMEM((rows, width), BF16),
            pltpu.VMEM((rows, width), BF16),
            pltpu.VMEM((rows * heads_all, HEAD_DIM), F32),
            pltpu.VMEM((n, lc * heads_all, HEAD_DIM), F32),
            pltpu.VMEM((8, 128), F32),
            pltpu.VMEM((n, 8, 128), F32),
            pltpu.VMEM((heads_all, HEAD_DIM), F32),
            pltpu.VMEM((lc * HEADS, HEAD_DIM), BF16),
            pltpu.VMEM((n, lc * HEADS, HEAD_DIM), BF16),
            pltpu.VMEM((rows * HEADS, HEAD_DIM), F32),
            pltpu.VMEM((rows, inner), BF16),
            pltpu.VMEM((n, rows, width), BF16),
            pltpu.VMEM((8, 128), F32),
            pltpu.VMEM((n, 8, 128), F32),
            pltpu.VMEM((8, 128), F32),
            pltpu.VMEM((total, 8, 128), F32),
            dma((chunks,)),
            dma((3,)),
            dma((n,)),
            dma((n,)),
            dma((n,)),
            dma((n,)),
            dma((n,)),
            dma((n,)),
            dma,
            dma,
            dma((n,)),
            dma((n,)),
            dma((n,)),
            dma((n,)),
            dma((2 * sections,)),
            dma((2,)),
            dma((total,)),
            dma((total,)),
        ],
        compiler_params=pltpu.CompilerParams(
            collective_id=0, has_side_effects=True, vmem_limit_bytes=60 * 1024 * 1024
        ),
    )(
        hidden_in,
        lengths.reshape(1, rows),
        assign.reshape(1, rows),
        token_ids.reshape(1, rows),
        attn_gain,
        qkv_weight,
        qkv_bias,
        out_weight,
        kv_cache,
        final_gain.reshape(1, width),
        head_weight,
        freq,
    )
    return logprobs, chosen[0, :rows]


def solution(mesh):
    return jax.shard_map(
        local,
        mesh=mesh,
        in_specs=(
            P(None, "mp"),
            P(),
            P(),
            P(),
            P("pipe", "mp"),
            P("pipe", "mp", None),
            P("pipe", None),
            P("pipe", None, "mp"),
            P("pipe", "mp", None, None, None, None),
            P("mp"),
            P(None, ("pipe", "mp")),
        ),
        out_specs=(P(None, ("pipe", "mp")), P()),
        check_vma=False,
    )
```

time: 1340 us -> 139 us (0.10)
  waiting for transfers between devices: 836 us -> 0 us
  blocking collectives: 276 us -> 0 us
  Pallas kernels: 0 us -> 134 us
  matrix products: 102 us -> 0 us
  local copies, waits for them, and re-layouts: 43.2 us -> 3.84 us
  starting transfers between devices: 35.9 us -> 0 us
  loops' own time: 22.4 us -> 0 us
  between operations: 15.3 us -> 0.64 us
    psum x8 -> x0, waiting for transfers between devices: 530 us -> none  [the longest x7 497 us: apply_layer(): gathered = lax.psum(spread.astype(jnp.bfloat16), 'mp')]
    reduce_scatter x7 -> x0, waiting for transfers between devices: 257 us -> none  [apply_layer(): lax.psum_scatter(partial_cols, 'mp', scatter_dimension=1, tiled=True)]
    psum x9 -> x0, blocking collectives: 207 us -> none  [the longest x7 145 us: apply_layer(): squares_all = lax.psum(squares, 'mp')]
    pallas_call x0 -> x1, Pallas kernels: none -> 134 us  [local(): pl.pallas_call(functools.partial(kernel, sections, n), out_shape=(jax.Sha...]
    dot_general x41 -> x0, matrix products: 102 us -> none  [the longest x7 42.7 us: apply_layer(): jnp.dot(scaled, weight_in, preferred_element_type=jnp.float32)]
    all_to_all x7 -> x0, waiting for transfers between devices: 48.7 us -> none  [apply_layer(): lax.all_to_all(routed_rows, 'mp', split_axis=0, concat_axis=1, tiled=True)]
    pmax x1 -> x0, blocking collectives: 36.8 us -> none  [local(): row_top = lax.pmax(local_top, ('pipe', 'mp'))]
    all_gather x1 -> x0, blocking collectives: 31.4 us -> none  [local(): lax.all_gather(normed, 'mp', axis=1, tiled=True)]
  transfers between devices with their start and end apart: 29 -> 0, of which waited for: 22 -> 0; matrix products, arithmetic and copies ran while one was open for 1% -> 0% of each run, Pallas kernels for 0% -> 0%
where the time goes in v1:
time: 139 us
  Pallas kernels  134 us (96%)
  local copies, waits for them, and re-layouts  3.84 us (3%)
    pallas_call x1, Pallas kernels, local(): pl.pallas_call(functools.partial(kernel, sections, n), out_shape=(jax.Sha...  134 us

profile of v1, /device:TPU:0, one launch (start us, length us, event | category | flops | bytes accessed | tf_op | source)
XLA Modules:
  0.0 138.8 jit_solution(7952063867256967795)
XLA Ops:
  0.6 1.3 reshape.19.final_gain
  1.9 134.3 %shard_map.131 = (f32[32,384]{1,0:T(8,128)}, f32[1,128]{1,0:T(1,128)}) custom-call(bf16[32,1024]{1,0:T(8,128)(2,1)} %hidden.1, s32[1,32]{1,0:T(1,128)} %bitcast.5, s32[1,32]{1,0:T(1,128)} %bitcast.6, s32[1,32]{1,0:T(1,128)} %bitcast.7, bf16[1,1024]{1,0:T(2,128)(2,1)} %gain.1, bf16[1,1024,5120]{2,1,0:T(8,128)(2,1)} %qkv_weight.1, bf16[1,5120]{1,0:T(2,128)(2,1)} %bias.1, ...), custom_call_target="tpu_custom_call" | custom-call | tf_op jit(solution)/shard_map/pallas_call | solution.py:448
  136.3 1.1 slice_bitcast_fusion
  137.4 1.4 %copy.15 = f32[32,384]{1,0:T(8,128)} copy(f32[32,384]{1,0:T(8,128)} %get-tuple-element.8) | data formatting | bytes 98304

commit v2 on v1

--- a/solution.py
+++ b/solution.py
@@ -53,17 +53,17 @@
     x,
     xo,
     scaled,
+    stage,
     part,
     part_in,
     sq,
     sq_in,
     bias_rows,
+    fresh,
     att,
     att_in,
-    att_rows,
-    att_mat,
+    update,
     fin,
-    fsq,
     fsq_in,
     red,
     red_in,
@@ -79,6 +79,8 @@
     hop_r,
     fin_s,
     fin_r,
+    sib_s,
+    sib_r,
     fsq_s,
     fsq_r,
     fp_s,
@@ -93,23 +95,33 @@
     lc = kv.shape[0]
     heads_all = HEADS + 2 * KV_HEADS
     group = HEADS // KV_HEADS
+    phases = heads_all // group
+    span = lc * group
     last = sections - 1
     scale = HEAD_DIM ** (-0.5)
-    chunks = wq_sem.shape[0]
-    cw = wq.shape[1] // chunks
+    cw = group * HEAD_DIM
+    half = rows // 2
+    core = lax.rem(sec, 2)
+    sibling = sec + 1 - 2 * core
 
     def wq_copy(c):
         cols = pl.ds(pl.multiple_of(c * cw, cw), cw)
         return pltpu.make_async_copy(qkv_weight.at[0, :, cols], wq.at[:, cols], wq_sem.at[c])
 
-    for c in range(chunks):
-        wq_copy(c).start()
+    def phase_of(k):
+        return lax.rem(k + phases - 1, phases)
+
+    for k in range(phases):
+        wq_copy((k + phases - 1) % phases).start()
     kv_copy = pltpu.make_async_copy(cache.at[0], kv, w_sem.at[0])
     wo_copy = pltpu.make_async_copy(out_weight.at[0], wo, w_sem.at[1])
     hw_copy = pltpu.make_async_copy(head_weight, hw, w_sem.at[2])
-    kv_copy.start()
-    wo_copy.start()
-    hw_copy.start()
+
+    @pl.when(sec > 0)
+    def _():
+        kv_copy.start()
+        wo_copy.start()
+        hw_copy.start()
 
     barrier = pltpu.get_barrier_semaphore()
     mine = sec * n + me
@@ -175,74 +187,107 @@
     )
     scaled[...] = (current * gain[...].astype(F32)).astype(BF16)
 
-    def sq_copy(peer, slot, sem):
-        return remote(sq, sq_in.at[slot], sq_s.at[peer], sq_r.at[sem], (sec, peer))
+    def sq_copy(peer, slot):
+        return remote(sq, sq_in.at[slot], sq_s.at[peer], sq_r.at[slot], (sec, peer))
+
+    def to_peer(k):
+        return lax.rem(me + k, n)
 
     for k in range(1, n):
-        peer = lax.rem(me + k, n)
-        sq_copy(peer, me, me).start()
-
-    per = cw // HEAD_DIM
-
-    def project(c, carry):
-        wq_copy(c).wait()
-        cols = pl.ds(pl.multiple_of(c * cw, cw), cw)
-        piece = jnp.dot(scaled[...], wq[:, cols], preferred_element_type=F32)
-        for j in range(per):
-            part[pl.ds(c * per + j, rows, stride=heads_all), :] = piece[
+        sq_copy(to_peer(k), me).start()
+    sq_in[me] = sq[...]
+
+    def part_copy(phase, peer, slot):
+        return remote(
+            part.at[phase, peer],
+            part_in.at[phase, slot],
+            part_s.at[phase, peer],
+            part_r.at[phase, slot],
+            (sec, peer),
+        )
+
+    def project(k, carry):
+        phase = phase_of(k)
+        wq_copy(phase).wait()
+        base = pl.multiple_of(phase * cw, cw)
+        piece = jnp.dot(scaled[...], wq[:, pl.ds(base, cw)], preferred_element_type=F32)
+        for j in range(group):
+            stage[pl.ds(j, rows, stride=group), :] = piece[
                 :, j * HEAD_DIM : (j + 1) * HEAD_DIM
             ]
-        return carry
-
-    lax.fori_loop(0, chunks, project, 0)
-
-    block = lc * heads_all
-
-    def part_copy(peer, slot):
-        return remote(
-            part.at[pl.ds(pl.multiple_of(peer * block, block), block), :],
-            part_in.at[slot],
-            part_s.at[peer],
-            part_r.at[slot],
-            (sec, peer),
-        )
+        for p in range(n):
+            part[phase, p] = stage[p * span : (p + 1) * span, :].astype(BF16)
+        for k in range(1, n):
+            part_copy(phase, to_peer(k), me).start()
+        part_in[phase, me] = part[phase, me]
+        return carry
+
+    lax.fori_loop(0, phases, project, 0)
+
+    @pl.when(sec == 0)
+    def _():
+        kv_copy.start()
+        wo_copy.start()
+        hw_copy.start()
+
+    def from_peer(k):
+        return lax.rem(me + n - k, n)
+
+    def summed(phase):
+        for k in range(1, n):
+            peer = from_peer(k)
+            part_copy(phase, peer, peer).wait_recv()
+        result = part_in[phase, 0].astype(F32)
+        for p in range(1, n):
+            result = result + part_in[phase, p].astype(F32)
+        return result
 
     for k in range(1, n):
-        part_copy(lax.rem(me + k, n), me).start()
-
-    squares = sq[...]
-    for k in range(1, n):
-        peer = lax.rem(me + n - k, n)
-        sq_copy(peer, peer, peer).wait_recv()
-        squares = squares + sq_in[peer]
-    summed_cols = part[pl.ds(pl.multiple_of(me * block, block), block), :]
-    for k in range(1, n):
-        peer = lax.rem(me + n - k, n)
-        part_copy(peer, peer).wait_recv()
-        summed_cols = summed_cols + part_in[peer]
-    kv_copy.wait()
-    pos = lax.broadcasted_iota(jnp.int32, (1, kv.shape[3]), 1).astype(F32)
-    for i in range(lc):
-        mean = (
+        peer = from_peer(k)
+        sq_copy(peer, peer).wait_recv()
+    squares = sq_in[0]
+    for p in range(1, n):
+        squares = squares + sq_in[p]
+    factor = [
+        lax.rsqrt(
             jnp.sum(
                 jnp.where(lane == me * lc + i, squares[0:1, :], 0.0), axis=1, keepdims=True
             )
             / (n * width)
-        )
-        rows_i = summed_cols[i * heads_all : (i + 1) * heads_all] * lax.rsqrt(
-            mean + EPS
-        ) + bias_rows[...]
-        turned = (
-            rows_i * cosine[i : i + 1]
-            + pltpu.roll(rows_i, HEAD_DIM // 2, 1) * sine[i : i + 1]
-        )
-        visible = pos < own_len[i]
-        heads = []
-        for h in range(KV_HEADS):
-            query = turned[h * group : (h + 1) * group].astype(BF16)
-            key_new = turned[HEADS + h : HEADS + h + 1].astype(BF16).astype(F32)
-            at = HEADS + KV_HEADS + h
-            value_new = rows_i[at : at + 1].astype(BF16).astype(F32)
+            + EPS
+        )
+        for i in range(lc)
+    ]
+
+    def turn(block, i):
+        return (
+            block * cosine[i : i + 1]
+            + pltpu.roll(block, HEAD_DIM // 2, 1) * sine[i : i + 1]
+        )
+
+    is_key = lax.broadcasted_iota(jnp.int32, (2 * KV_HEADS, HEAD_DIM), 0) < KV_HEADS
+    block_sum = summed(phases - 1)
+    for i in range(lc):
+        block = block_sum[i * group : (i + 1) * group] * factor[i] + bias_rows[HEADS:, :]
+        fresh[i] = jnp.where(is_key, turn(block, i), block).astype(BF16).astype(F32)
+    kv_copy.wait()
+    pos = lax.broadcasted_iota(jnp.int32, (1, kv.shape[3]), 1).astype(F32)
+
+    def att_copy(h, peer, slot):
+        return remote(
+            att.at[h], att_in.at[h, slot], att_s.at[h, peer], att_r.at[h, slot], (sec, peer)
+        )
+
+    def attend(h, carry):
+        block_sum = summed(h)
+        bias_h = bias_rows[pl.ds(pl.multiple_of(h * group, group), group), :]
+        done = []
+        for i in range(lc):
+            block = block_sum[i * group : (i + 1) * group] * factor[i] + bias_h
+            query = turn(block, i).astype(BF16)
+            key_new = fresh[i, pl.ds(h, 1), :]
+            value_new = fresh[i, pl.ds(KV_HEADS + h, 1), :]
+            visible = pos < own_len[i]
             scores = (
                 lax.dot_general(
                     query,
@@ -263,34 +308,33 @@
             denominator = jnp.sum(weights, axis=1, keepdims=True) + self_weight
             mixed = jnp.dot(weights.astype(BF16), kv[i, 1, h], preferred_element_type=F32)
             mixed = mixed + self_weight.astype(BF16).astype(F32) * value_new
-            heads.append(mixed / denominator)
-        att[i * HEADS : (i + 1) * HEADS, :] = jnp.concatenate(heads, axis=0).astype(BF16)
-
-    def att_copy(peer, slot):
-        return remote(att, att_in.at[slot], att_s.at[peer], att_r.at[slot], (sec, peer))
-
-    for k in range(1, n):
-        att_copy(lax.rem(me + k, n), me).start()
-    span = lc * HEADS
-    att_rows[pl.ds(pl.multiple_of(me * span, span), span), :] = att[...].astype(F32)
-    for k in range(1, n):
-        peer = lax.rem(me + n - k, n)
-        att_copy(peer, peer).wait_recv()
-        att_rows[pl.ds(pl.multiple_of(peer * span, span), span), :] = att_in[peer].astype(F32)
-    for i in range(HEADS):
-        att_mat[:, i * HEAD_DIM : (i + 1) * HEAD_DIM] = att_rows[
-            pl.ds(i, rows, stride=HEADS), :
-        ].astype(BF16)
+            done.append(mixed / denominator)
+        att[h] = jnp.concatenate(done, axis=0).astype(BF16)
+        for k in range(1, n):
+            att_copy(h, to_peer(k), me).start()
+        att_in[h, me] = att[h]
+        return carry
+
+    lax.fori_loop(0, KV_HEADS, attend, 0)
     wo_copy.wait()
-    ow = min(256, width)
-
-    def project_out(c, carry):
-        cols = pl.ds(pl.multiple_of(c * ow, ow), ow)
-        update = jnp.dot(att_mat[...], wo[:, cols], preferred_element_type=F32)
-        xo[:, cols] = (x[:, cols].astype(F32) + update).astype(BF16)
-        return carry
-
-    lax.fori_loop(0, width // ow, project_out, 0)
+    update[...] = x[...].astype(F32)
+
+    def project_out(h, carry):
+        for k in range(1, n):
+            peer = from_peer(k)
+            att_copy(h, peer, peer).wait_recv()
+        for p in range(n):
+            stage[p * span : (p + 1) * span, :] = att_in[h, p].astype(F32)
+        mat = jnp.concatenate(
+            [stage[pl.ds(j, rows, stride=group), :].astype(BF16) for j in range(group)],
+            axis=1,
+        )
+        depth = pl.ds(pl.multiple_of(h * cw, cw), cw)
+        update[...] += jnp.dot(mat, wo[depth, :], preferred_element_type=F32)
+        return carry
+
+    lax.fori_loop(0, KV_HEADS, project_out, 0)
+    xo[...] = update[...].astype(BF16)
 
     @pl.when(sec < last)
     def _():
@@ -298,33 +342,42 @@
         hop.start()
         hop.wait_send()
 
-    def fin_pipe(k, from_here):
+    def fin_pipe(k):
         to = lax.rem(sec + k, sections)
-        dev = (to, me)
+        piece = lax.rem(to, 2)
         return (
-            remote(fin.at[me], fin.at[me], fp_s.at[2 * k], fp_r.at[0], dev),
-            remote(fsq_in.at[me], fsq_in.at[me], fp_s.at[2 * k + 1], fp_r.at[1], dev),
+            remote(fin.at[piece, me], fin.at[piece, me], fp_s.at[2 * k], fp_r.at[0], (to, me)),
+            remote(fsq_in.at[me], fsq_in.at[me], fp_s.at[2 * k + 1], fp_r.at[1], (to, me)),
         )
 
     @pl.when(sec == last)
     def _():
         final = jnp.dot(order.astype(BF16), xo[...], preferred_element_type=F32)
-        fin[me] = (final * final_gain[...].astype(F32)).astype(BF16)
+        both = (final * final_gain[...].astype(F32)).astype(BF16)
+        fin[0, me] = both[:half]
+        fin[1, me] = both[half:]
         fsq_in[me] = jnp.broadcast_to(
-            to_row(jnp.sum(final * final, axis=1, keepdims=True)), fsq.shape
+            to_row(jnp.sum(final * final, axis=1, keepdims=True)), (8, 128)
         )
         for k in range(1, sections):
-            for copy in fin_pipe(k, True):
+            for copy in fin_pipe(k):
                 copy.start()
 
     @pl.when(sec < last)
     def _():
-        for copy in fin_pipe(1, False):
-            copy.wait_recv()
+        arriving = remote(fin.at[core, me], fin.at[core, me], fp_s.at[0], fp_r.at[0], (last, me))
+        arriving.wait_recv()
+        arriving = remote(fsq_in.at[me], fsq_in.at[me], fp_s.at[1], fp_r.at[1], (last, me))
+        arriving.wait_recv()
 
     def fin_copy(peer, slot):
         return remote(
-            fin.at[slot], fin.at[slot], fin_s.at[peer], fin_r.at[slot], (sec, peer)
+            fin.at[core, slot], fin.at[core, slot], fin_s.at[peer], fin_r.at[slot], (sec, peer)
+        )
+
+    def sib_copy(piece, slot):
+        return remote(
+            fin.at[piece, slot], fin.at[piece, slot], sib_s.at[slot], sib_r.at[slot], (sibling, me)
         )
 
     def fsq_copy(peer, slot):
@@ -333,27 +386,55 @@
         )
 
     for k in range(1, n):
-        peer = lax.rem(me + k, n)
-        fin_copy(peer, me).start()
-        fsq_copy(peer, me).start()
+        fin_copy(to_peer(k), me).start()
+    for k in range(1, n):
+        fsq_copy(to_peer(k), me).start()
+
+    @pl.when(sec < last - 1)
+    def _():
+        sib_copy(core, me).start()
+
+    @pl.when(sec == last - 1)
+    def _():
+        mate = remote(fin.at[1 - core, me], fin.at[1 - core, me], fp_s.at[0], fp_r.at[2], (last, me))
+        mate.wait_recv()
+
+    @pl.when(sec == last)
+    def _():
+        mate = remote(
+            fin.at[core, me], fin.at[core, me], sib_s.at[me], fp_r.at[2], (sibling, me)
+        )
+        mate.start()
+
+    for k in range(1, n):
+        peer = from_peer(k)
+        fin_copy(peer, peer).wait_recv()
+        sib_copy(core, peer).start()
+
+    @pl.when(sec < last - 1)
+    def _():
+        sib_copy(1 - core, me).wait_recv()
+
     hw_copy.wait()
 
     def head(k, logits):
-        peer = lax.rem(me + n - k, n)
+        peer = from_peer(k)
 
         @pl.when(k > 0)
         def _():
-            fin_copy(peer, peer).wait_recv()
+            sib_copy(1 - core, peer).wait_recv()
 
         rows_at = pl.ds(pl.multiple_of(peer * width, width), width)
-        return logits + jnp.dot(fin[peer], hw[rows_at, :], preferred_element_type=F32)
+        both = jnp.concatenate([fin[0, peer], fin[1, peer]], axis=0)
+        return logits + jnp.dot(both, hw[rows_at, :], preferred_element_type=F32)
 
     logits = lax.fori_loop(0, n, head, jnp.zeros(out.shape, F32))
-    squares = fsq_in[me]
     for k in range(1, n):
-        peer = lax.rem(me + n - k, n)
+        peer = from_peer(k)
         fsq_copy(peer, peer).wait_recv()
-        squares = squares + fsq_in[peer]
+    squares = fsq_in[0]
+    for p in range(1, n):
+        squares = squares + fsq_in[p]
     logits = logits * lax.rsqrt(to_col(squares[0:1, :]) / (n * width) + EPS)
     vocab = out.shape[1]
     ids = (mine * vocab + lax.broadcasted_iota(jnp.int32, (1, vocab), 1)).astype(F32)
@@ -393,18 +474,28 @@
     chosen[...] = jnp.sum(red_in[:, 2, :], axis=0, keepdims=True) - log_total
     out[...] = logits - to_col(log_total)
 
-    for k in range(1, n):
-        peer = lax.rem(me + k, n)
-        sq_copy(peer, me, me).wait_send()
-        part_copy(peer, me).wait_send()
-        att_copy(peer, me).wait_send()
+    def peer_done(k, carry):
+        peer = to_peer(k)
+        sq_copy(peer, me).wait_send()
+        for phase in range(phases):
+            part_copy(phase, peer, me).wait_send()
+        for h in range(KV_HEADS):
+            att_copy(h, peer, me).wait_send()
         fin_copy(peer, me).wait_send()
         fsq_copy(peer, me).wait_send()
+        sib_copy(core, peer).wait_send()
+        return carry
+
+    lax.fori_loop(1, n, peer_done, 0)
+
+    @pl.when(sec != last - 1)
+    def _():
+        sib_copy(core, me).wait_send()
 
     @pl.when(sec == last)
     def _():
         for k in range(1, sections):
-            for copy in fin_pipe(k, True):
+            for copy in fin_pipe(k):
                 copy.wait_send()
 
     def red_done(k, carry):
@@ -440,7 +531,9 @@
         -np.arange(half).astype(np.float32) * np.float32(2.0) / np.float32(HEAD_DIM)
     )
     freq = jnp.asarray(np.concatenate([frequency, frequency])[None, :], F32)
-    chunks = qkv // 512
+    group = HEADS // KV_HEADS
+    phases = heads_all // group
+    span = lc * group
     dma = pltpu.SemaphoreType.DMA
     vm = pl.BlockSpec(memory_space=pltpu.VMEM)
     hbm = pl.BlockSpec(memory_space=pl.ANY)
@@ -461,36 +554,38 @@
             pltpu.VMEM((rows, width), BF16),
             pltpu.VMEM((rows, width), BF16),
             pltpu.VMEM((rows, width), BF16),
-            pltpu.VMEM((rows * heads_all, HEAD_DIM), F32),
-            pltpu.VMEM((n, lc * heads_all, HEAD_DIM), F32),
+            pltpu.VMEM((rows * group, HEAD_DIM), F32),
+            pltpu.VMEM((phases, n, span, HEAD_DIM), BF16),
+            pltpu.VMEM((phases, n, span, HEAD_DIM), BF16),
             pltpu.VMEM((8, 128), F32),
             pltpu.VMEM((n, 8, 128), F32),
             pltpu.VMEM((heads_all, HEAD_DIM), F32),
-            pltpu.VMEM((lc * HEADS, HEAD_DIM), BF16),
-            pltpu.VMEM((n, lc * HEADS, HEAD_DIM), BF16),
-            pltpu.VMEM((rows * HEADS, HEAD_DIM), F32),
-            pltpu.VMEM((rows, inner), BF16),
-            pltpu.VMEM((n, rows, width), BF16),
-            pltpu.VMEM((8, 128), F32),
+            pltpu.VMEM((lc, 2 * KV_HEADS, HEAD_DIM), F32),
+            pltpu.VMEM((KV_HEADS, span, HEAD_DIM), BF16),
+            pltpu.VMEM((KV_HEADS, n, span, HEAD_DIM), BF16),
+            pltpu.VMEM((rows, width), F32),
+            pltpu.VMEM((2, n, rows // 2, width), BF16),
             pltpu.VMEM((n, 8, 128), F32),
             pltpu.VMEM((8, 128), F32),
             pltpu.VMEM((total, 8, 128), F32),
-            dma((chunks,)),
+            dma((phases,)),
             dma((3,)),
-            dma((n,)),
-            dma((n,)),
-            dma((n,)),
-            dma((n,)),
-            dma((n,)),
-            dma((n,)),
+            dma((phases, n)),
+            dma((phases, n)),
+            dma((n,)),
+            dma((n,)),
+            dma((KV_HEADS, n)),
+            dma((KV_HEADS, n)),
             dma,
             dma,
             dma((n,)),
             dma((n,)),
             dma((n,)),
             dma((n,)),
+            dma((n,)),
+            dma((n,)),
             dma((2 * sections,)),
-            dma((2,)),
+            dma((3,)),
             dma((total,)),
             dma((total,)),
         ],

time: 139 us -> 95.3 us (0.69)
  Pallas kernels: 134 us -> 90.6 us
    pallas_call x1, Pallas kernels: 134 us -> 90.6 us  [local(): pl.pallas_call(functools.partial(kernel, sections, n), out_shape=(jax.Sha...]
where the time goes in v2:
time: 95.3 us; the launch traced here: 95.1 us
  Pallas kernels  90.6 us (95%)
  local copies, waits for them, and re-layouts  3.84 us (4%)
    pallas_call x1, Pallas kernels, local(): pl.pallas_call(functools.partial(kernel, sections, n), out_shape=(jax.Sha...  90.6 us

profile of v2, /device:TPU:0, one launch (start us, length us, event | category | flops | bytes accessed | tf_op | source)
XLA Modules:
  0.0 95.1 jit_solution(2836630971417719817)
XLA Ops:
  0.6 1.3 %reshape.19.final_gain = bf16[1,1024]{1,0:T(2,128)(2,1)} reshape(bf16[1024]{0:T(1024)(128)(2,1)} %param.21) | data formatting | bytes 4096 | tf_op jit(solution)/shard_map/reshape | solution.py:605
  1.9 90.6 %shard_map.131 = (f32[32,384]{1,0:T(8,128)}, f32[1,128]{1,0:T(1,128)}) custom-call(bf16[32,1024]{1,0:T(8,128)(2,1)} %hidden.1, s32[1,32]{1,0:T(1,128)} %bitcast.5, s32[1,32]{1,0:T(1,128)} %bitcast.6, s32[1,32]{1,0:T(1,128)} %bitcast.7, bf16[1,1024]{1,0:T(2,128)(2,1)} %gain.1, bf16[1,1024,5120]{2,1,0:T(8,128)(2,1)} %qkv_weight.1, bf16[1,5120]{1,0:T(2,128)(2,1)} %bias.1, ...), custom_call_target="tpu_custom_call" | custom-call | tf_op jit(solution)/shard_map/pallas_call | solution.py:541
  92.5 1.1 %slice_bitcast_fusion = f32[32]{0:T(128)} fusion(f32[1,128]{1,0:T(1,128)} %get-tuple-element.5), kind=kLoop, calls=%fused_computation | loop fusion | bytes 256 | tf_op jit(solution)/shard_map/squeeze | solution.py:609
  93.6 1.4 %copy.15 = f32[32,384]{1,0:T(8,128)} copy(f32[32,384]{1,0:T(8,128)} %get-tuple-element.8) | data formatting | bytes 98304

commit v3 on v2

--- a/solution.py
+++ b/solution.py
@@ -208,6 +208,11 @@
 
     def project(k, carry):
         phase = phase_of(k)
+
+        @pl.when((sec == 0) & (k == 2))
+        def _():
+            kv_copy.start()
+
         wq_copy(phase).wait()
         base = pl.multiple_of(phase * cw, cw)
         piece = jnp.dot(scaled[...], wq[:, pl.ds(base, cw)], preferred_element_type=F32)
@@ -226,7 +231,6 @@
 
     @pl.when(sec == 0)
     def _():
-        kv_copy.start()
         wo_copy.start()
         hw_copy.start()
 
@@ -278,44 +282,53 @@
             att.at[h], att_in.at[h, slot], att_s.at[h, peer], att_r.at[h, slot], (sec, peer)
         )
 
-    def attend(h, carry):
-        block_sum = summed(h)
-        bias_h = bias_rows[pl.ds(pl.multiple_of(h * group, group), group), :]
-        done = []
-        for i in range(lc):
-            block = block_sum[i * group : (i + 1) * group] * factor[i] + bias_h
-            query = turn(block, i).astype(BF16)
-            key_new = fresh[i, pl.ds(h, 1), :]
-            value_new = fresh[i, pl.ds(KV_HEADS + h, 1), :]
-            visible = pos < own_len[i]
-            scores = (
-                lax.dot_general(
-                    query,
-                    kv[i, 0, h],
-                    (((1,), (1,)), ((), ())),
-                    preferred_element_type=F32,
+    together = 2
+
+    def attend(step, carry):
+        sums = [summed(step * together + u) for u in range(together)]
+        for u in range(together):
+            h = step * together + u
+            bias_h = bias_rows[pl.ds(pl.multiple_of(h * group, group), group), :]
+            done = []
+            for i in range(lc):
+                block = sums[u][i * group : (i + 1) * group] * factor[i] + bias_h
+                query = turn(block, i).astype(BF16)
+                key_new = fresh[i, pl.ds(h, 1), :]
+                value_new = fresh[i, pl.ds(KV_HEADS + h, 1), :]
+                visible = pos < own_len[i]
+                scores = (
+                    lax.dot_general(
+                        query,
+                        kv[i, 0, h],
+                        (((1,), (1,)), ((), ())),
+                        preferred_element_type=F32,
+                    )
+                    * scale
                 )
-                * scale
-            )
-            self_score = (
-                jnp.sum(query.astype(F32) * key_new, axis=1, keepdims=True) * scale
-            )
-            top = jnp.maximum(
-                jnp.max(jnp.where(visible, scores, -1e30), axis=1, keepdims=True), self_score
-            )
-            weights = jnp.where(visible, jnp.exp(scores - top), 0.0)
-            self_weight = jnp.exp(self_score - top)
-            denominator = jnp.sum(weights, axis=1, keepdims=True) + self_weight
-            mixed = jnp.dot(weights.astype(BF16), kv[i, 1, h], preferred_element_type=F32)
-            mixed = mixed + self_weight.astype(BF16).astype(F32) * value_new
-            done.append(mixed / denominator)
-        att[h] = jnp.concatenate(done, axis=0).astype(BF16)
-        for k in range(1, n):
-            att_copy(h, to_peer(k), me).start()
-        att_in[h, me] = att[h]
-        return carry
-
-    lax.fori_loop(0, KV_HEADS, attend, 0)
+                self_score = (
+                    jnp.sum(query.astype(F32) * key_new, axis=1, keepdims=True) * scale
+                )
+                top = jnp.maximum(
+                    jnp.max(jnp.where(visible, scores, -1e30), axis=1, keepdims=True),
+                    self_score,
+                )
+                weights = jnp.where(visible, jnp.exp(scores - top), 0.0)
+                self_weight = jnp.exp(self_score - top)
+                denominator = jnp.sum(weights, axis=1, keepdims=True) + self_weight
+                mixed = jnp.dot(
+                    weights.astype(BF16), kv[i, 1, h], preferred_element_type=F32
+                )
+                mixed = mixed + self_weight.astype(BF16).astype(F32) * value_new
+                done.append(mixed / denominator)
+            att[h] = jnp.concatenate(done, axis=0).astype(BF16)
+            att_in[h, me] = att[h]
+        for u in range(together):
+            h = step * together + u
+            for k in range(1, n):
+                att_copy(h, to_peer(k), me).start()
+        return carry
+
+    lax.fori_loop(0, KV_HEADS // together, attend, 0)
     wo_copy.wait()
     update[...] = x[...].astype(F32)
 
@@ -353,7 +366,7 @@
     @pl.when(sec == last)
     def _():
         final = jnp.dot(order.astype(BF16), xo[...], preferred_element_type=F32)
-        both = (final * final_gain[...].astype(F32)).astype(BF16)
+        both = (final * final_gain[...].astype(F32)[None, :]).astype(BF16)
         fin[0, me] = both[:half]
         fin[1, me] = both[half:]
         fsq_in[me] = jnp.broadcast_to(
@@ -602,7 +615,7 @@
         qkv_bias,
         out_weight,
         kv_cache,
-        final_gain.reshape(1, width),
+        final_gain,
         head_weight,
         freq,
     )

time: 95.3 us -> 97 us (1.018)
  Pallas kernels: 90.6 us -> 93.6 us
  local copies, waits for them, and re-layouts: 3.84 us -> 2.57 us
    pallas_call x1, Pallas kernels: 90.6 us -> 93.6 us  [local(): pl.pallas_call(functools.partial(kernel, sections, n), out_shape=(jax.Sha...]
    reshape x1 -> x0, local copies, waits for them, and re-layouts: 1.28 us -> none  [local(): final_gain.reshape(1, width)]
where the time goes in v3:
time: 97 us; the launch traced here: 96.8 us
  Pallas kernels  93.6 us (96%)
  local copies, waits for them, and re-layouts  2.57 us (3%)
    pallas_call x1, Pallas kernels, local(): pl.pallas_call(functools.partial(kernel, sections, n), out_shape=(jax.Sha...  93.6 us

profile of v3, /device:TPU:0, one launch (start us, length us, event | category | flops | bytes accessed | tf_op | source)
XLA Modules:
  0.0 96.8 jit_solution(5555514275024424795)
XLA Ops:
  0.6 93.6 %shard_map.131 = (f32[32,384]{1,0:T(8,128)}, f32[1,128]{1,0:T(1,128)}) custom-call(bf16[32,1024]{1,0:T(8,128)(2,1)} %hidden.1, s32[1,32]{1,0:T(1,128)} %bitcast.5, s32[1,32]{1,0:T(1,128)} %bitcast.6, s32[1,32]{1,0:T(1,128)} %bitcast.7, bf16[1,1024]{1,0:T(2,128)(2,1)} %gain.1, bf16[1,1024,5120]{2,1,0:T(8,128)(2,1)} %qkv_weight.1, bf16[1,5120]{1,0:T(2,128)(2,1)} %bias.1, ...), custom_call_target="tpu_custom_call" | custom-call | tf_op jit(solution)/shard_map/pallas_call | solution.py:554
  94.2 1.1 %slice_bitcast_fusion = f32[32]{0:T(128)} fusion(f32[1,128]{1,0:T(1,128)} %get-tuple-element.5), kind=kLoop, calls=%fused_computation | loop fusion | bytes 256 | tf_op jit(solution)/shard_map/squeeze | solution.py:622
  95.4 1.4 %copy.15 = f32[32,384]{1,0:T(8,128)} copy(f32[32,384]{1,0:T(8,128)} %get-tuple-element.8) | data formatting | bytes 98304
